TPU v7x, 256 devices: a whole 4x4x8 slice. The times are simulated.
256 devices in a mesh: group: 4 (over x), dp: 16 (over z_lo, y, core), mp: 4 (over z_hi).
Axes of the slice: x: 4, y: 4, z: 8 (z_hi: 4, z_lo: 2; z = z_hi * 2 + z_lo), core: 2. Of those that a mesh axis runs over, the one named last changes fastest.
Arguments:
- block_input: bfloat16 [768, 8192], P(None, 'dp'), may hold values from -6 to 6
- parent_gate_up: bfloat16 [2, 8192, 14336], P(None, 'dp', ('group', 'mp')), may hold values from -0.0625 to 0.0625
- parent_down: bfloat16 [14336, 8192], P(('group', 'mp'), 'dp'), may hold values from -0.046875 to 0.046875
- variant_gate_up: bfloat16 [4, 2, 8192, 3584], P('group', None, 'dp', 'mp'), may hold values from -0.0625 to 0.0625
- variant_down: bfloat16 [4, 3584, 8192], P('group', 'mp', 'dp'), may hold values from -0.09375 to 0.09375
- widths: int32 [4], P('group'), may hold values from 896 to 3584, as said below
Outputs:
- grad_gate_up: float32 [4, 2, 8192, 3584], P('group', None, 'dp', 'mp')
- grad_down: float32 [4, 3584, 8192], P('group', 'mp', 'dp')
Inputs may be any that keep to these rules, and one draw needn't show every extreme that they name: Variant v uses its hidden units 0 to widths[v] - 1; one variant uses all 3584 of them and another exactly a quarter of 3584.
All inputs are finite; a program needn't handle non-finite values.
Results may differ from a plain program's by a relative error of at most 0.008.
Values may be sent and summed in bfloat16 or wider, within the bound.
No kernel may reach another device: no remote copies, remote signals or barrier semaphores. Data moves between devices by JAX's collectives and lax.ppermute only.
A program may use at most 64 MiB of HBM per device.

v0:
```python
import math
import jax
import jax.numpy as jnp
from jax import lax
from jax.sharding import PartitionSpec as P


def gated_values(pre_act, unit_mask):
    gate_value = pre_act[:, 0].astype(jnp.float32)
    up_value = pre_act[:, 1].astype(jnp.float32)
    sigmoid_gate = jax.nn.sigmoid(gate_value)
    return (gate_value * sigmoid_gate * up_value * unit_mask).astype(jnp.bfloat16)


def pre_gradient(pre_act, unit_mask, hidden_grad):
    gate_value = pre_act[:, 0].astype(jnp.float32)
    up_value = pre_act[:, 1].astype(jnp.float32)
    sigmoid_gate = jax.nn.sigmoid(gate_value)
    masked_grad = hidden_grad * unit_mask
    grad_gate = masked_grad * up_value * sigmoid_gate * (1.0 + gate_value * (1.0 - sigmoid_gate))
    grad_up = masked_grad * gate_value * sigmoid_gate
    return jnp.stack([grad_gate, grad_up], axis=1).astype(jnp.bfloat16)


def body(block_input, parent_gate_up, parent_down, variant_gate_up, variant_down, widths):
    local_gate_up = variant_gate_up[0]
    local_down = variant_down[0]
    local_units = local_down.shape[0]
    all_tokens = block_input.shape[0]
    first_unit = lax.axis_index("mp") * local_units
    unit_index = first_unit + jnp.arange(local_units, dtype=jnp.int32)
    unit_mask = (unit_index < widths[0]).astype(jnp.float32)
    parent_term = jnp.einsum(
        "td,kdf->tkf", block_input, parent_gate_up, preferred_element_type=jnp.float32
    )
    variant_term = jnp.einsum(
        "td,kdf->tkf", block_input, local_gate_up, preferred_element_type=jnp.float32
    )
    parent_rows, variant_rows = (
        lax.psum_scatter(parent_term, "dp", scatter_dimension=0, tiled=True),
        lax.psum_scatter(variant_term, "dp", scatter_dimension=0, tiled=True),
    )
    parent_pre = parent_rows.astype(jnp.bfloat16)
    variant_pre = variant_rows.astype(jnp.bfloat16)
    parent_hidden = gated_values(parent_pre, 1.0)
    parent_all, variant_all = (
        lax.all_gather(parent_hidden, "dp", axis=0, tiled=True),
        lax.all_gather(variant_pre, "dp", axis=0, tiled=True),
    )
    variant_hidden = gated_values(variant_all, unit_mask)
    teacher_part = jnp.dot(parent_all, parent_down, preferred_element_type=jnp.float32)
    student_part = jnp.dot(variant_hidden, local_down, preferred_element_type=jnp.float32)
    teacher = lax.psum(teacher_part, ("group", "mp"))
    student = lax.psum(student_part, "mp")
    loss_scale = 1.0 / math.sqrt(all_tokens)
    output_grad = ((student - teacher) * loss_scale).astype(jnp.bfloat16)
    grad_down = lax.dot_general(
        variant_hidden, output_grad, (((0,), (0,)), ((), ())), preferred_element_type=jnp.float32
    )
    hidden_part = lax.dot_general(
        output_grad, local_down, (((1,), (1,)), ((), ())), preferred_element_type=jnp.float32
    )
    hidden_full = lax.psum(hidden_part, "dp")
    grad_pre = pre_gradient(variant_all, unit_mask, hidden_full)
    grad_gate_up = jnp.einsum(
        "td,tkf->kdf", block_input, grad_pre, preferred_element_type=jnp.float32
    )
    return (grad_gate_up[None], grad_down[None])


def solution(mesh):
    in_specs = (
        P(None, "dp"),
        P(None, "dp", ("group", "mp")),
        P(("group", "mp"), "dp"),
        P("group", None, "dp", "mp"),
        P("group", "mp", "dp"),
        P("group"),
    )
    out_specs = (P("group", None, "dp", "mp"), P("group", "mp", "dp"))
    return jax.shard_map(body, mesh=mesh, in_specs=in_specs, out_specs=out_specs, check_vma=False)
```

profile of v0, /device:TPU:1, one launch (start us, length us, event | category | flops | bytes accessed | tf_op | source)
XLA Modules:
  0.0 652.1 jit_solution(2625803845936884595)
XLA Ops:
  7.2 0.0 copy-start
  7.2 0.0 reduce-scatter.5.cloned.1.call-start
  7.2 1.4 copy-done
  8.7 5.2 fusion.45
  13.9 0.0 copy-start.1
  13.9 0.0 reduce-scatter.5.cloned.1.call-update
  13.9 0.0 reduce-scatter.3.cloned.1.call-start
  13.9 1.1 copy-done.1
  15.0 5.5 fusion.29
  20.5 0.0 reduce-scatter.3.cloned.1.call-update
  20.5 0.0 all-gather.5.cloned.1.call-start
  20.6 66.0 %reduce-scatter.5.cloned.1.call-done = f32[48,2,896]{2,0,1:T(8,128)} async-done(((f32[768,2,896]{2,0,1:T(8,128)}), f32[48,2,896]{2,0,1:T(8,128)}) %reduce-scatter.5.cloned.1.call-update) | async-done | bytes 344080 | tf_op jit(solution)/shard_map/reduce_scatter | solution.py:40
  86.6 1.0 convert_element_type.66
  87.6 0.7 fusion.52
  88.3 0.0 all-gather.5.cloned.1.call-update
  88.3 0.0 all-gather.3.cloned.1.call-start
  88.4 71.3 %reduce-scatter.3.cloned.1.call-done = f32[48,2,896]{2,0,1:T(8,128)} async-done(((f32[768,2,896]{2,0,1:T(8,128)}), f32[48,2,896]{2,0,1:T(8,128)}) %reduce-scatter.3.cloned.1.call-update) | async-done | bytes 344080 | tf_op jit(solution)/shard_map/reduce_scatter | solution.py:41
  159.7 1.7 convert_element_type.60
  161.3 0.0 all-gather.3.cloned.1.call-update
  161.3 0.0 copy-start.2
  161.4 0.0 all-reduce.6.cloned.1.call-start
  161.4 38.0 %all-gather.5.cloned.1.call-done = bf16[768,896]{1,0:T(8,128)(2,1)} async-done(((bf16[48,896]{1,0:T(8,128)(2,1)}), bf16[768,896]{1,0:T(8,128)(2,1)}) %all-gather.5.cloned.1.call-update) | async-done | bytes 1376272 | tf_op jit(solution)/shard_map/all_gather | solution.py:47
  199.4 3.7 fusion.57
  203.1 0.0 all-reduce.6.cloned.1.call-update
  203.1 0.0 all-reduce.4.cloned.1.call-start
  203.8 35.3 %all-gather.3.cloned.1.call-done = bf16[768,2,896]{2,0,1:T(8,128)(2,1)} async-done(((bf16[48,2,896]{2,0,1:T(8,128)(2,1)}), bf16[768,2,896]{2,0,1:T(8,128)(2,1)}) %all-gather.3.cloned.1.call-update) | async-done | bytes 2752528 | tf_op jit(solution)/shard_map/all_gather | solution.py:48
  239.1 0.0 copy-done.2
  239.1 4.0 fusion.31
  243.2 0.0 all-reduce.4.cloned.1.call-update
  243.2 0.0 all-reduce.8.cloned.1.call-start
  243.2 163.2 %all-reduce.6.cloned.1.call-done = f32[768,512]{1,0:T(8,128)} async-done(((f32[768,512]{1,0:T(8,128)}), f32[768,512]{1,0:T(8,128)}) %all-reduce.6.cloned.1.call-update) | async-done | bytes 1572880 | tf_op jit(solution)/shard_map/psum | solution.py:53
  406.4 93.0 %all-reduce.4.cloned.1.call-done = f32[768,512]{1,0:T(8,128)} async-done(((f32[768,512]{1,0:T(8,128)}), f32[768,512]{1,0:T(8,128)}) %all-reduce.4.cloned.1.call-update) | async-done | bytes 1572880 | tf_op jit(solution)/shard_map/psum | solution.py:54
  499.4 2.3 multiply_convert_fusion
  501.7 3.7 fusion.39
  505.4 0.0 all-reduce.8.cloned.1.call-update
  505.5 4.1 convolution_bitcast_fusion
  509.6 123.6 %all-reduce.8.cloned.1.call-done = f32[768,896]{1,0:T(8,128)} async-done(((f32[768,896]{1,0:T(8,128)}), f32[768,896]{1,0:T(8,128)}) %all-reduce.8.cloned.1.call-update) | async-done | bytes 2752528 | tf_op jit(solution)/shard_map/psum | solution.py:63
  633.2 4.0 fusion.36
  637.2 3.5 fusion.26
  640.7 4.6 copy.9
  (1 shorter events, 0.0 us)
Async XLA Ops:
  7.2 1.5 copy-start
  7.2 79.4 %reduce-scatter.5.cloned.1.call-start = ((), (), s32[]{:S(2)}) async-start(), calls=%async_computation.5 | async-start | bytes 5849088 | tf_op jit(solution)/shard_map/reduce_scatter | solution.py:40
  13.9 1.1 copy-start.1
  13.9 145.8 %reduce-scatter.3.cloned.1.call-start = ((), (), s32[]{:S(2)}) async-start(), calls=%async_computation.2 | async-start | bytes 5849088 | tf_op jit(solution)/shard_map/reduce_scatter | solution.py:41
  20.5 178.9 %all-gather.5.cloned.1.call-start = ((), (), s32[]{:S(2)}) async-start(), calls=%async_computation.6 | async-start | bytes 1462272 | tf_op jit(solution)/shard_map/all_gather | solution.py:47
  88.3 150.8 %all-gather.3.cloned.1.call-start = ((), (), s32[]{:S(2)}) async-start(), calls=%async_computation.3 | async-start | bytes 2924544 | tf_op jit(solution)/shard_map/all_gather | solution.py:48
  161.3 77.8 %copy-start.2 = (bf16[1,896,512]{2,1,0:T(8,128)(2,1)S(1)}, bf16[1,896,512]{2,1,0:T(8,128)(2,1)}, u32[]{:S(2)}) copy-start(bf16[1,896,512]{2,1,0:T(8,128)(2,1)} %param.10) | copy-start | bytes 2752516
  161.4 245.1 %all-reduce.6.cloned.1.call-start = ((), (), s32[]{:S(2)}) async-start(), calls=%async_computation.7 | async-start | bytes 3145728 | tf_op jit(solution)/shard_map/psum | solution.py:53
  203.1 296.3 %all-reduce.4.cloned.1.call-start = ((), (), s32[]{:S(2)}) async-start(), calls=%async_computation.4 | async-start | bytes 3145728 | tf_op jit(solution)/shard_map/psum | solution.py:54
  243.2 390.0 %all-reduce.8.cloned.1.call-start = ((), (), s32[]{:S(2)}) async-start(), calls=%async_computation.8 | async-start | bytes 5505024 | tf_op jit(solution)/shard_map/psum | solution.py:63
Sparse Core Ops, SparseCore 0:
  14.0 72.5 reduce-scatter.4
  89.1 70.4 reduce-scatter.2
  162.1 37.2 all-gather.4
  201.6 37.4 all-gather.2
  242.2 164.1 all-reduce.5
  409.5 89.8 all-reduce.3
  505.6 127.5 all-reduce.7
where the time goes:
time: 653 us; the launch traced here: 652 us
  waiting for transfers between devices  590 us (90%)
  matrix products  29.8 us (5%)
  between operations  14.8 us (2%)
  other arithmetic  9.67 us (1%)
  local copies, waits for them, and re-layouts  7.1 us (1%)
    psum x1, waiting for transfers between devices, body(): teacher = lax.psum(teacher_part, ('group', 'mp'))  163 us
    psum x1, waiting for transfers between devices, body(): hidden_full = lax.psum(hidden_part, 'dp')  124 us
    psum x1, waiting for transfers between devices, body(): student = lax.psum(student_part, 'mp')  93 us
    reduce_scatter x1, waiting for transfers between devices, body(): lax.psum_scatter(variant_term, 'dp', scatter_dimension=0, tiled=True)  71.3 us
    reduce_scatter x1, waiting for transfers between devices, body(): lax.psum_scatter(parent_term, 'dp', scatter_dimension=0, tiled=True)  66 us
    all_gather x1, waiting for transfers between devices, body(): lax.all_gather(parent_hidden, 'dp', axis=0, tiled=True)  38 us
    all_gather x1, waiting for transfers between devices, body(): lax.all_gather(variant_pre, 'dp', axis=0, tiled=True)  35.3 us
  transfers between devices with their start and end apart: 7, of which 7 were waited for; matrix products, arithmetic and copies ran while one was open for 3% of the time, Pallas kernels for 0%

commit v1 on v0

--- a/solution.py
+++ b/solution.py
@@ -51,7 +51,7 @@
     teacher_part = jnp.dot(parent_all, parent_down, preferred_element_type=jnp.float32)
     student_part = jnp.dot(variant_hidden, local_down, preferred_element_type=jnp.float32)
     teacher = lax.psum(teacher_part, ("group", "mp"))
-    student = lax.psum(student_part, "mp")
+    student = jnp.sum(jax.lax.all_gather(student_part, "mp"), 0)
     loss_scale = 1.0 / math.sqrt(all_tokens)
     output_grad = ((student - teacher) * loss_scale).astype(jnp.bfloat16)
     grad_down = lax.dot_general(

time: 653 us -> 690 us (1.057)
  waiting for transfers between devices: 590 us -> 623 us
    all_gather x0 -> x1, waiting for transfers between devices: none -> 117 us  [body(): student = jnp.sum(jax.lax.all_gather(student_part, 'mp'), 0)]
    psum x1 -> x0, waiting for transfers between devices: 93 us -> none  [body(): student = lax.psum(student_part, 'mp')]
    psum x1, waiting for transfers between devices: 124 us -> 131 us  [body(): hidden_full = lax.psum(hidden_part, 'dp')]
  transfers between devices with their start and end apart: 7 -> 7, of which waited for: 7 -> 7; matrix products, arithmetic and copies ran while one was open for 3% -> 4% of each run, Pallas kernels for 0% -> 0%
where the time goes in v1:
time: 690 us; the launch traced here: 689 us
  waiting for transfers between devices  623 us (90%)
  matrix products  28.5 us (4%)
  between operations  14.8 us (2%)
  other arithmetic  13 us (2%)
  local copies, waits for them, and re-layouts  9.08 us (1%)
    psum x1, waiting for transfers between devices, body(): teacher = lax.psum(teacher_part, ('group', 'mp'))  164 us
    psum x1, waiting for transfers between devices, body(): hidden_full = lax.psum(hidden_part, 'dp')  131 us
    all_gather x1, waiting for transfers between devices, body(): student = jnp.sum(jax.lax.all_gather(student_part, 'mp'), 0)  117 us
    reduce_scatter x1, waiting for transfers between devices, body(): lax.psum_scatter(parent_term, 'dp', scatter_dimension=0, tiled=True)  71.3 us
    reduce_scatter x1, waiting for transfers between devices, body(): lax.psum_scatter(variant_term, 'dp', scatter_dimension=0, tiled=True)  66 us
    all_gather x1, waiting for transfers between devices, body(): lax.all_gather(variant_pre, 'dp', axis=0, tiled=True)  39.5 us
    all_gather x1, waiting for transfers between devices, body(): lax.all_gather(parent_hidden, 'dp', axis=0, tiled=True)  33.6 us
  transfers between devices with their start and end apart: 7, of which 7 were waited for; matrix products, arithmetic and copies ran while one was open for 4% of the time, Pallas kernels for 0%

profile of v1, /device:TPU:1, one launch (start us, length us, event | category | flops | bytes accessed | tf_op | source)
XLA Modules:
  0.0 689.2 jit_solution(12115107575456486976)
XLA Ops:
  7.2 0.0 copy-start
  7.2 0.0 reduce-scatter.3.cloned.1.call-start
  7.2 1.4 copy-done
  8.7 5.2 fusion.29
  13.8 0.0 copy-start.3
  13.8 0.0 reduce-scatter.3.cloned.1.call-update
  13.9 0.0 reduce-scatter.5.cloned.1.call-start
  13.9 1.1 copy-done.3
  15.0 5.5 fusion.45
  20.5 0.0 copy-start.5
  20.5 0.0 reduce-scatter.5.cloned.1.call-update
  20.5 0.0 all-gather.5.cloned.1.call-start
  20.5 66.0 %reduce-scatter.3.cloned.1.call-done = f32[48,2,896]{2,0,1:T(8,128)} async-done(((f32[768,2,896]{2,0,1:T(8,128)}), f32[48,2,896]{2,0,1:T(8,128)}) %reduce-scatter.3.cloned.1.call-update) | async-done | bytes 344080 | tf_op jit(solution)/shard_map/reduce_scatter | solution.py:41
  86.6 1.7 convert_element_type.60
  88.2 0.0 all-gather.5.cloned.1.call-update
  88.3 0.0 all-gather.7.cloned.1.call-start
  88.3 71.3 %reduce-scatter.5.cloned.1.call-done = f32[48,2,896]{2,0,1:T(8,128)} async-done(((f32[768,2,896]{2,0,1:T(8,128)}), f32[48,2,896]{2,0,1:T(8,128)}) %reduce-scatter.5.cloned.1.call-update) | async-done | bytes 344080 | tf_op jit(solution)/shard_map/reduce_scatter | solution.py:40
  159.6 1.0 convert_element_type.66
  160.6 0.7 fusion.52
  161.3 0.0 all-gather.7.cloned.1.call-update
  161.4 0.0 all-gather.9.cloned.1.call-start
  162.1 39.5 %all-gather.5.cloned.1.call-done = bf16[768,2,896]{2,0,1:T(8,128)(2,1)} async-done(((bf16[48,2,896]{2,0,1:T(8,128)(2,1)}), bf16[768,2,896]{2,0,1:T(8,128)(2,1)}) %all-gather.5.cloned.1.call-update) | async-done | bytes 2752528 | tf_op jit(solution)/shard_map/all_gather | solution.py:48
  201.6 0.0 copy-done.5
  201.6 4.0 fusion.31
  205.6 0.0 all-gather.9.cloned.1.call-update
  205.6 0.0 all-reduce.3.cloned.1.call-start
  205.7 33.6 %all-gather.7.cloned.1.call-done = bf16[768,896]{1,0:T(8,128)(2,1)} async-done(((bf16[48,896]{1,0:T(8,128)(2,1)}), bf16[768,896]{1,0:T(8,128)(2,1)}) %all-gather.7.cloned.1.call-update) | async-done | bytes 1376272 | tf_op jit(solution)/shard_map/all_gather | solution.py:47
  239.3 3.7 fusion.57
  243.0 0.0 all-reduce.3.cloned.1.call-update
  243.0 0.0 all-reduce.5.cloned.1.call-start
  243.1 117.2 %all-gather.9.cloned.1.call-done = f32[3072,512]{1,0:T(8,128)} async-done(((f32[768,512]{1,0:T(8,128)}), f32[3072,512]{1,0:T(8,128)}) %all-gather.9.cloned.1.call-update) | async-done | bytes 6291472 | tf_op jit(solution)/shard_map/all_gather | solution.py:54
  360.2 3.7 reduce_sum.9
  363.9 164.3 %all-reduce.3.cloned.1.call-done = f32[768,512]{1,0:T(8,128)} async-done(((f32[768,512]{1,0:T(8,128)}), f32[768,512]{1,0:T(8,128)}) %all-reduce.3.cloned.1.call-update) | async-done | bytes 1572880 | tf_op jit(solution)/shard_map/psum | solution.py:53
  528.2 0.0 copy-start.6
  528.2 1.9 multiply_convert_fusion
  530.1 0.0 copy-start.1
  530.1 0.9 copy-done.1
  531.0 0.0 copy-done.6
  531.0 2.5 fusion.39
  533.5 0.0 copy-start.2
  533.5 0.0 all-reduce.5.cloned.1.call-update
  533.6 1.1 copy-done.2
  534.7 4.1 convolution_bitcast_fusion
  538.8 0.0 copy-start.4
  538.8 131.5 %all-reduce.5.cloned.1.call-done = f32[768,896]{1,0:T(8,128)} async-done(((f32[768,896]{1,0:T(8,128)}), f32[768,896]{1,0:T(8,128)}) %all-reduce.5.cloned.1.call-update) | async-done | bytes 2752528 | tf_op jit(solution)/shard_map/psum | solution.py:63
  670.3 4.0 fusion.36
  674.3 0.0 copy-done.4
  674.3 3.5 fusion.26
  677.7 4.6 copy.9
  (1 shorter events, 0.0 us)
Async XLA Ops:
  7.2 1.5 copy-start
  7.2 79.4 %reduce-scatter.3.cloned.1.call-start = ((), (), s32[]{:S(2)}) async-start(), calls=%async_computation.2 | async-start | bytes 5849088 | tf_op jit(solution)/shard_map/reduce_scatter | solution.py:41
  13.8 1.1 copy-start.3
  13.9 145.8 %reduce-scatter.5.cloned.1.call-start = ((), (), s32[]{:S(2)}) async-start(), calls=%async_computation.4 | async-start | bytes 5849088 | tf_op jit(solution)/shard_map/reduce_scatter | solution.py:40
  20.5 181.1 %copy-start.5 = (bf16[1,896,512]{2,1,0:T(8,128)(2,1)S(1)}, bf16[1,896,512]{2,1,0:T(8,128)(2,1)}, u32[]{:S(2)}) copy-start(bf16[1,896,512]{2,1,0:T(8,128)(2,1)} %param.10) | copy-start | bytes 2752516
  20.5 181.1 %all-gather.5.cloned.1.call-start = ((), (), s32[]{:S(2)}) async-start(), calls=%async_computation.3 | async-start | bytes 2924544 | tf_op jit(solution)/shard_map/all_gather | solution.py:48
  88.3 151.0 %all-gather.7.cloned.1.call-start = ((), (), s32[]{:S(2)}) async-start(), calls=%async_computation.5 | async-start | bytes 1462272 | tf_op jit(solution)/shard_map/all_gather | solution.py:47
  161.4 198.9 %all-gather.9.cloned.1.call-start = ((), (), s32[]{:S(2)}) async-start(), calls=%async_computation.8 | async-start | bytes 7864320 | tf_op jit(solution)/shard_map/all_gather | solution.py:54
  205.6 322.6 %all-reduce.3.cloned.1.call-start = ((), (), s32[]{:S(2)}) async-start(), calls=%async_computation.6 | async-start | bytes 3145728 | tf_op jit(solution)/shard_map/psum | solution.py:53
  243.0 427.2 %all-reduce.5.cloned.1.call-start = ((), (), s32[]{:S(2)}) async-start(), calls=%async_computation.7 | async-start | bytes 5505024 | tf_op jit(solution)/shard_map/psum | solution.py:63
  528.2 2.8 copy-start.6
  530.1 0.9 copy-start.1
  533.5 1.1 copy-start.2
  538.8 135.5 %copy-start.4 = (bf16[768,512]{1,0:T(8,128)(2,1)S(1)}, bf16[768,512]{1,0:T(8,128)(2,1)}, u32[]{:S(2)}) copy-start(bf16[768,512]{1,0:T(8,128)(2,1)} %param.6) | copy-start | bytes 2359300
Sparse Core Ops, SparseCore 0:
  14.0 72.5 reduce-scatter.2
  89.1 70.4 reduce-scatter.4
  162.0 39.5 all-gather.4
  203.9 35.3 all-gather.6
  241.5 118.6 all-gather.8
  363.3 164.8 all-reduce.2
  533.7 136.5 all-reduce.4
